TPU v7x, 8 devices: a whole 2x2x1 slice. The times are simulated.
8 devices in a mesh: dp: 1 (over z), tp: 8 (over x, y, core).
Axes of the slice: x: 2, y: 2, z: 1, core: 2. Of those that a mesh axis runs over, the one named last changes fastest.
Arguments:
- x: bfloat16 [2048, 5120], P('dp')
- w_gate: bfloat16 [5120, 16384], P(None, 'tp')
- w_up: bfloat16 [5120, 16384], P(None, 'tp')
- w_down: bfloat16 [16384, 5120], P('tp')
Outputs:
- output: bfloat16 [2048, 5120], P('dp')
All inputs are finite; a program needn't handle non-finite values.
Results may differ from a plain program's by a relative error of at most 0.016.
Values are sent between devices in bfloat16 or wider.
A program may use at most 2 GiB of HBM per device.

v0:
```python
import jax
import jax.numpy as jnp
from jax import lax
from jax.sharding import PartitionSpec as P


def solution(mesh):
    def step(x, w_gate, w_up, w_down):
        gate = jnp.dot(x, w_gate, preferred_element_type=jnp.float32)
        up = jnp.dot(x, w_up, preferred_element_type=jnp.float32)
        hidden = (jax.nn.silu(gate) * up).astype(jnp.bfloat16)
        term = jnp.dot(hidden, w_down, preferred_element_type=jnp.float32).astype(jnp.bfloat16)
        return lax.psum(term, "tp")

    return jax.shard_map(
        step,
        mesh=mesh,
        in_specs=(P("dp", None), P(None, "tp"), P(None, "tp"), P("tp", None)),
        out_specs=P("dp", None),
        check_vma=False,
    )
```

profile of v0, /device:TPU:0, one launch (start us, length us, event | category | flops | bytes accessed | tf_op | source)
XLA Modules:
  0.0 447.3 jit_solution(11275783865051270504)
XLA Ops:
  6.5 0.0 all-reduce.2.cloned.1.call-start
  6.5 52.9 %fusion = f32[2048,2048]{1,0:T(8,128)} fusion(bf16[2048,5120]{1,0:T(8,128)(2,1)} %param.4, bf16[5120,2048]{1,0:T(8,128)(2,1)} %param.5), kind=kOutput, calls=%fused_computation.2 | convolution fusion | flops 42949672960 | bytes 58720256 | tf_op jit(solution)/shard_map/dot_general | solution.py:9
  59.4 58.3 %multiply_convert_fusion = bf16[2048,2048]{1,0:T(8,128)(2,1)} fusion(f32[2048,2048]{1,0:T(8,128)} %fusion, bf16[2048,5120]{1,0:T(8,128)(2,1)} %param.4, bf16[5120,2048]{1,0:T(8,128)(2,1)} %param.6), kind=kOutput, calls=%fused_computation.1 | convolution fusion | flops 42974838784 | bytes 67108864 | tf_op jit(solution)/shard_map/dot_general | solution.py:10
  117.7 51.2 %convolution_convert_fusion = bf16[2048,5120]{1,0:T(8,128)(2,1)} fusion(bf16[2048,2048]{1,0:T(8,128)(2,1)} %multiply_convert_fusion, bf16[2048,5120]{1,0:T(8,128)(2,1)} %param.7), kind=kOutput, calls=%fused_computation | convolution fusion | flops 42960158720 | bytes 50331648 | tf_op jit(solution)/shard_map/dot_general | solution.py:12
  168.9 0.0 all-reduce.2.cloned.1.call-update
  168.9 254.3 %all-reduce.2.cloned.1.call-done = bf16[2048,5120]{1,0:T(8,128)(2,1)} async-done(((bf16[2048,5120]{1,0:T(8,128)(2,1)}), bf16[2048,5120]{1,0:T(8,128)(2,1)}) %all-reduce.2.cloned.1.call-update) | async-done | bytes 20971536 | tf_op jit(solution)/shard_map/psum | solution.py:13
  423.2 17.3 %copy.6 = bf16[2048,5120]{1,0:T(8,128)(2,1)} copy(bf16[2048,5120]{1,0:T(8,128)(2,1)} %all-reduce.2.cloned.1.call-done) | data formatting | bytes 41943040
Async XLA Ops:
  6.5 416.6 %all-reduce.2.cloned.1.call-start = ((), (), s32[]{:S(2)}) async-start(), calls=%async_computation | async-start | bytes 41943040 | tf_op jit(solution)/shard_map/psum | solution.py:13
Sparse Core Ops, SparseCore 0:
  169.0 254.1 all-reduce.1
where the time goes:
time: 447 us
  waiting for transfers between devices  254 us (57%)
  matrix products  162 us (36%)
  local copies, waits for them, and re-layouts  17.3 us (4%)
  between operations  13.4 us (3%)
    psum x1, waiting for transfers between devices, step(): return lax.psum(term, 'tp')  254 us
    dot_general x1, matrix products, step(): up = jnp.dot(x, w_up, preferred_element_type=jnp.float32)  58.3 us
    dot_general x1, matrix products, step(): gate = jnp.dot(x, w_gate, preferred_element_type=jnp.float32)  52.9 us
    dot_general x1, matrix products, step(): jnp.dot(hidden, w_down, preferred_element_type=jnp.float32)  51.2 us
    unnamed x1, local copies, waits for them, and re-layouts  17.3 us
  transfers between devices with their start and end apart: 1, of which 1 were waited for; matrix products, arithmetic and copies ran while one was open for 0% of the time, Pallas kernels for 0%

commit v1 on v0

v1 whole, which is shorter than its diff:
```python
import functools

import jax
import jax.numpy as jnp
from jax import lax
from jax.experimental import pallas as pl
from jax.experimental.pallas import tpu as pltpu
from jax.sharding import PartitionSpec as P

MESH = pl.DeviceIdType.MESH
R = 256
GT = 512
F32, BF16 = jnp.float32, jnp.bfloat16


def _dot(a, b):
    return jnp.dot(a, b, preferred_element_type=F32)


def kernel(
    x_ref, wg_ref, wu_ref, wd_ref, t_ref,
    xb, wg, wd, ring, hb, s0s, s0r, s1s, s1r, s2s, s2r, keep1, keep2, fin,
    x_sem, wg_sem, wd_sem, ring_sem,
    s0_ss, s0_rs, s1_ss, s1_rs, s2_ss, s2_rs,
    ag_ss, ag_rs, loc_sem,
    credit0, credit1, credit2,
):
    rows, d = x_ref.shape
    hid = wg_ref.shape[1]
    nc = rows // R
    nt = hid // GT
    kh = d // 2
    blk = d // 8
    nring = 3

    me = lax.axis_index("tp")
    c = lax.rem(me, 2)
    cy = lax.rem(me // 2, 2)
    cx = me // 4
    k1 = cx + c * (cy - cx)
    k2 = cy + c * (cx - cy)
    partner = me + 1 - 2 * c
    n1 = me + (1 - 2 * k1) * (4 - 2 * c)
    n2 = me + (1 - 2 * k2) * (2 + 2 * c)

    mine = 4 * c + 2 * k1 + k2
    mine_n2 = 4 * c + 2 * k1 + (1 - k2)
    far_a = 4 * c + 2 * (1 - k1) + k2
    far_b = 4 * c + 2 * (1 - k1) + (1 - k2)
    pc = 4 * (1 - c)
    p_mine = pc + 2 * k2 + k1
    p_mine_n2 = pc + 2 * k2 + (1 - k1)
    p_far = pc + 2 * (1 - k2)

    def tile(j, b, n=1):
        return t_ref.at[pl.ds(pl.multiple_of(j * R, R), R), pl.ds(pl.multiple_of(b * blk, 128), n * blk)]

    def remote(src, dst, ss, rs, to):
        return pltpu.make_async_remote_copy(
            src_ref=src, dst_ref=dst, send_sem=ss, recv_sem=rs, device_id={"tp": to}, device_id_type=MESH
        )

    def load_x(i):
        return pltpu.make_async_copy(x_ref.at[pl.ds(pl.multiple_of(i * R, R), R)], xb, x_sem)

    def load_g(t):
        return pltpu.make_async_copy(wg_ref.at[:, pl.ds(pl.multiple_of(t * GT, 128), GT)], wg.at[t], wg_sem.at[t])

    order = (
        2 * (1 - c) + (1 - k2),
        2 * c + (1 - k1),
        2 * (1 - c) + k2,
        2 * c + k1,
    )

    def load_d(o):
        col = pl.multiple_of(order[o] * (2 * blk), 128)
        return pltpu.make_async_copy(wd_ref.at[:, pl.ds(col, 2 * blk)], wd.at[o], wd_sem.at[o])

    def load_u(g):
        s = lax.rem(g, 2 * nt)
        t, half = s // 2, lax.rem(s, 2)
        slot = lax.rem(g, nring)
        src = wu_ref.at[pl.ds(pl.multiple_of(half * kh, kh), kh), pl.ds(pl.multiple_of(t * GT, 128), GT)]
        return pltpu.make_async_copy(src, ring.at[slot], ring_sem.at[slot])

    def s0(b):
        return remote(s0s.at[b], s0r.at[b], s0_ss.at[b], s0_rs.at[b], partner)

    def s1(j):
        p = lax.rem(j, 2)
        return remote(s1s.at[p], s1r.at[p], s1_ss.at[p], s1_rs.at[p], n1)

    def s2(j):
        p = lax.rem(j, 2)
        return remote(s2s.at[p], s2r.at[p], s2_ss.at[p], s2_rs.at[p], n2)

    def ag(kind, j, src, dst, to):
        return remote(src, dst, ag_ss.at[kind, j], ag_rs.at[kind, j], to)

    def fins(j):
        f = fin.at[lax.rem(j, 2)]
        dst = tile(j, mine)
        return (
            ag(0, j, f, dst, n2),
            ag(1, j, f, dst, n1),
            ag(2, j, f, dst, partner),
            pltpu.make_async_copy(f, dst, loc_sem.at[lax.rem(j, 2)]),
        )

    def wait_fins(j):
        a1, a2, a0, loc = fins(j)
        a1.wait_send()
        a2.wait_send()
        a0.wait_send()
        loc.wait()

    def passed(j):
        v = tile(j, mine_n2)
        return ag(3, j, v, v, n1), ag(4, j, v, v, partner)

    def crossed(j):
        v = tile(j, 4 * c + 2 * (1 - k1), 2)
        return ag(5, j, v, v, partner)

    def event1(j):
        s1(j).wait_recv()
        p = lax.rem(j, 2)

        @pl.when(j >= 2)
        def _():
            s2(j).wait_send()
            pl.semaphore_wait(credit2, 1)

        s2s[p] = (keep1[1 - k2] + s1r[p, 1 - k2].astype(F32)).astype(BF16)
        s2(j).start()
        keep2[...] = keep1[k2] + s1r[p, k2].astype(F32)

        @pl.when(j < nc - 2)
        def _():
            pl.semaphore_signal(credit1, inc=1, device_id={"tp": n1}, device_id_type=MESH)

    def event2(j):
        s2(j).wait_recv()
        p = lax.rem(j, 2)

        @pl.when(j >= 2)
        def _():
            wait_fins(j - 2)

        fin[p] = (keep2[...] + s2r[p].astype(F32)).astype(BF16)
        for cp in fins(j):
            cp.start()

        @pl.when(j < nc - 2)
        def _():
            pl.semaphore_signal(credit2, inc=1, device_id={"tp": n2}, device_id_type=MESH)

    def event3(j):
        v = tile(j, mine_n2)
        ag(0, j, v, v, n2).wait_recv()
        for cp in passed(j):
            cp.start()

    def event4(j):
        v = tile(j, far_a)
        ag(1, j, v, v, n1).wait_recv()
        v = tile(j, far_b)
        ag(3, j, v, v, n1).wait_recv()
        crossed(j).start()

    def finish(j):
        v = tile(j, p_mine)
        ag(2, j, v, v, partner).wait_recv()
        v = tile(j, p_mine_n2)
        ag(4, j, v, v, partner).wait_recv()
        v = tile(j, p_far, 2)
        ag(5, j, v, v, partner).wait_recv()
        for cp in passed(j):
            cp.wait_send()
        crossed(j).wait_send()

    load_x(0).start()
    load_g(0).start()
    load_u(0).start()
    load_u(1).start()
    load_g(1).start()
    load_u(2).start()

    barrier = pltpu.get_barrier_semaphore()
    for to in (partner, n1, n2):
        pl.semaphore_signal(barrier, inc=1, device_id={"tp": to}, device_id_type=MESH)
    pl.semaphore_wait(barrier, 3)

    def chunk(i, carry):
        load_x(i).wait()

        def gate_up(t, carry):
            g0 = 2 * nt * i + 2 * t

            @pl.when(i == 0)
            def _():
                load_g(t).wait()

                @pl.when(t < nt - 2)
                def _():
                    load_g(t + 2).start()

            gate = _dot(xb[...], wg[t])
            load_u(g0).wait()
            load_u(g0 + 1).wait()
            up = _dot(xb[:, :kh], ring[lax.rem(g0, nring)])
            up += _dot(xb[:, kh:], ring[lax.rem(g0 + 1, nring)])
            hb[:, pl.ds(pl.multiple_of(t * GT, 128), GT)] = (jax.nn.silu(gate) * up).astype(BF16)

            @pl.when(g0 + 3 < 2 * nt * nc)
            def _():
                load_u(g0 + 3).start()

            @pl.when(g0 + 4 < 2 * nt * nc)
            def _():
                load_u(g0 + 4).start()

            @pl.when((i == 0) & (t >= nt - 2))
            def _():
                for o in range(2):
                    @pl.when(t == nt - 2 + o)
                    def _():
                        load_d(o).start()

            @pl.when((i >= 1) & (t == 1))
            def _():
                @pl.when(i >= 2)
                def _():
                    event4(i - 2)

                event1(i - 1)

            @pl.when((i >= 1) & (t == nt - 1))
            def _():
                event2(i - 1)

            return carry

        lax.fori_loop(0, nt, gate_up, 0)

        @pl.when(i < nc - 1)
        def _():
            load_x(i + 1).start()

        for o in range(4):
            @pl.when(i == 0)
            def _():
                load_d(o).wait()
                if o < 2:
                    load_d(o + 2).start()

            b = o // 2
            if o % 2 == 0:
                @pl.when(i >= 1)
                def _():
                    s0(b).wait_send()
                    pl.semaphore_wait(credit0.at[b], 1)

                v = _dot(hb[...], wd[o]).astype(BF16)
                s0s[b, 0] = v[:, :blk]
                s0s[b, 1] = v[:, blk:]
                s0(b).start()
            else:
                v = _dot(hb[...], wd[o])
                s0(b).wait_recv()
                lo = v[:, :blk] + s0r[b, 0].astype(F32)
                hi = v[:, blk:] + s0r[b, 1].astype(F32)
                if o == 1:
                    @pl.when(i >= 2)
                    def _():
                        s1(i).wait_send()
                        pl.semaphore_wait(credit1, 1)

                    p = lax.rem(i, 2)
                    s1s[p, 0] = lo.astype(BF16)
                    s1s[p, 1] = hi.astype(BF16)
                    s1(i).start()
                else:
                    keep1[0] = lo
                    keep1[1] = hi

                @pl.when(i < nc - 1)
                def _():
                    pl.semaphore_signal(credit0.at[b], inc=1, device_id={"tp": partner}, device_id_type=MESH)

        @pl.when(i >= 1)
        def _():
            event3(i - 1)

        return carry

    lax.fori_loop(0, nc, chunk, 0)

    event1(nc - 1)
    event4(nc - 2)
    event2(nc - 1)
    event3(nc - 1)
    event4(nc - 1)
    for b in range(2):
        s0(b).wait_send()
    for j in (nc - 2, nc - 1):
        s1(j).wait_send()
        s2(j).wait_send()
        wait_fins(j)

    def last(j, carry):
        finish(j)
        return carry

    lax.fori_loop(0, nc, last, 0)


def block(x, wg, wu, wd):
    rows, d = x.shape
    hid = wg.shape[1]
    nc, blk = rows // R, d // 8
    hbm = pl.BlockSpec(memory_space=pl.ANY)
    dma, reg = pltpu.SemaphoreType.DMA, pltpu.SemaphoreType.REGULAR
    return pl.pallas_call(
        kernel,
        out_shape=jax.ShapeDtypeStruct((rows, d), BF16),
        in_specs=[hbm] * 4,
        out_specs=hbm,
        scratch_shapes=[
            pltpu.VMEM((R, d), BF16),
            pltpu.VMEM((hid // GT, d, GT), BF16),
            pltpu.VMEM((4, hid, 2 * blk), BF16),
            pltpu.VMEM((3, d // 2, GT), BF16),
            pltpu.VMEM((R, hid), BF16),
            pltpu.VMEM((2, 2, R, blk), BF16),
            pltpu.VMEM((2, 2, R, blk), BF16),
            pltpu.VMEM((2, 2, R, blk), BF16),
            pltpu.VMEM((2, 2, R, blk), BF16),
            pltpu.VMEM((2, R, blk), BF16),
            pltpu.VMEM((2, R, blk), BF16),
            pltpu.VMEM((2, R, blk), F32),
            pltpu.VMEM((R, blk), F32),
            pltpu.VMEM((2, R, blk), BF16),
            dma, dma((hid // GT,)), dma((4,)), dma((3,)),
            dma((2,)), dma((2,)), dma((2,)), dma((2,)), dma((2,)), dma((2,)),
            dma((6, nc)), dma((6, nc)), dma((2,)),
            reg((2,)), reg, reg,
        ],
        compiler_params=pltpu.CompilerParams(
            collective_id=0, has_side_effects=True, vmem_limit_bytes=67_043_328
        ),
        cost_estimate=pl.CostEstimate(
            flops=6 * rows * d * hid, bytes_accessed=2 * (12 * d * hid), transcendentals=rows * hid
        ),
        name="mlp_all_reduce",
    )(x, wg, wu, wd)


def solution(mesh):
    return jax.shard_map(
        block,
        mesh=mesh,
        in_specs=(P("dp", None), P(None, "tp"), P(None, "tp"), P("tp", None)),
        out_specs=P("dp", None),
        check_vma=False,
    )
```

time: 447 us -> 256 us (0.57)
  waiting for transfers between devices: 254 us -> 0 us
  Pallas kernels: 0 us -> 239 us
  matrix products: 162 us -> 0 us
  between operations: 13.4 us -> 0.01 us
    psum x1 -> x0, waiting for transfers between devices: 254 us -> none  [step(): return lax.psum(term, 'tp')]
    pallas_call x0 -> x1, Pallas kernels: none -> 239 us  [block(): pl.pallas_call(kernel, out_shape=jax.ShapeDtypeStruct((rows, d), BF16), i...]
    dot_general x3 -> x0, matrix products: 162 us -> none  [the longest x1 58.3 us: step(): up = jnp.dot(x, w_up, preferred_element_type=jnp.float32)]
  transfers between devices with their start and end apart: 1 -> 0, of which waited for: 1 -> 0; matrix products, arithmetic and copies ran while one was open for 0% -> 0% of each run, Pallas kernels for 0% -> 0%
where the time goes in v1:
time: 256 us
  Pallas kernels  239 us (93%)
  local copies, waits for them, and re-layouts  17.3 us (7%)
    pallas_call x1, Pallas kernels, block(): pl.pallas_call(kernel, out_shape=jax.ShapeDtypeStruct((rows, d), BF16), i...  239 us
    unnamed x1, local copies, waits for them, and re-layouts  17.3 us

profile of v1, /device:TPU:0, one launch (start us, length us, event | category | flops | bytes accessed | tf_op | source)
XLA Modules:
  0.0 256.2 jit_solution(15346965867765573532)
XLA Ops:
  0.0 238.9 %mlp_all_reduce.1 = bf16[2048,5120]{1,0:T(8,128)(2,1)} custom-call(bf16[2048,5120]{1,0:T(8,128)(2,1)} %x_ref.1, bf16[5120,2048]{1,0:T(8,128)(2,1)} %wg_ref.1, bf16[5120,2048]{1,0:T(8,128)(2,1)} %wu_ref.1, bf16[2048,5120]{1,0:T(8,128)(2,1)} %wd_ref.1), custom_call_target="tpu_custom_call" | custom-call | flops 128849018880 | bytes 251658240 | tf_op jit(solution)/shard_map/mlp_all_reduce/pallas_call | solution.py:325
  238.9 17.3 %copy.6 = bf16[2048,5120]{1,0:T(8,128)(2,1)} copy(bf16[2048,5120]{1,0:T(8,128)(2,1)} %mlp_all_reduce.1) | data formatting | bytes 41943040

commit v2 on v1

--- a/solution.py
+++ b/solution.py
@@ -12,18 +12,20 @@
 GT = 512
 F32, BF16 = jnp.float32, jnp.bfloat16
 
+EVENTS = ((3, 1, 2), (1, 2, 1), (4, 4, 3), (2, 5, 1))
+
 
 def _dot(a, b):
     return jnp.dot(a, b, preferred_element_type=F32)
 
 
 def kernel(
-    x_ref, wg_ref, wu_ref, wd_ref, t_ref,
-    xb, wg, wd, ring, hb, s0s, s0r, s1s, s1r, s2s, s2r, keep1, keep2, fin,
+    x_ref, wg_ref, wu_ref, wd_ref, y_ref, t_ref,
+    xb, wg, ring, hb, s0s, s0r, s1s, s1r, s2s, s2r, keep1, keep2, fin,
     x_sem, wg_sem, wd_sem, ring_sem,
     s0_ss, s0_rs, s1_ss, s1_rs, s2_ss, s2_rs,
-    ag_ss, ag_rs, loc_sem,
-    credit0, credit1, credit2,
+    ag_ss, ag_rs, loc_sem, fetch_sem,
+    credit0, credit1, credit2, free,
 ):
     rows, d = x_ref.shape
     hid = wg_ref.shape[1]
@@ -53,7 +55,8 @@
     p_far = pc + 2 * (1 - k2)
 
     def tile(j, b, n=1):
-        return t_ref.at[pl.ds(pl.multiple_of(j * R, R), R), pl.ds(pl.multiple_of(b * blk, 128), n * blk)]
+        ref = y_ref if isinstance(j, int) and j == nc - 1 else t_ref
+        return ref.at[pl.ds(pl.multiple_of(j * R, R), R), pl.ds(pl.multiple_of(b * blk, 128), n * blk)]
 
     def remote(src, dst, ss, rs, to):
         return pltpu.make_async_remote_copy(
@@ -75,7 +78,7 @@
 
     def load_d(o):
         col = pl.multiple_of(order[o] * (2 * blk), 128)
-        return pltpu.make_async_copy(wd_ref.at[:, pl.ds(col, 2 * blk)], wd.at[o], wd_sem.at[o])
+        return pltpu.make_async_copy(wd_ref.at[:, pl.ds(col, 2 * blk)], y_ref.at[:, pl.ds(o * 2 * blk, 2 * blk)], wd_sem.at[o])
 
     def load_u(g):
         s = lax.rem(g, 2 * nt)
@@ -149,6 +152,9 @@
             wait_fins(j - 2)
 
         fin[p] = (keep2[...] + s2r[p].astype(F32)).astype(BF16)
+        if isinstance(j, int) and j == nc - 1:
+            for b in range(3):
+                pl.semaphore_wait(free.at[b], 1)
         for cp in fins(j):
             cp.start()
 
@@ -169,7 +175,9 @@
         ag(3, j, v, v, n1).wait_recv()
         crossed(j).start()
 
-    def finish(j):
+    def event5(j):
+        if isinstance(j, int) and j >= nc - 2:
+            wait_fins(j)
         v = tile(j, p_mine)
         ag(2, j, v, v, partner).wait_recv()
         v = tile(j, p_mine_n2)
@@ -179,6 +187,15 @@
         for cp in passed(j):
             cp.wait_send()
         crossed(j).wait_send()
+        if not (isinstance(j, int) and j == nc - 1):
+            fetch(j).start()
+
+    def fetch(j):
+        rows_j = pl.ds(pl.multiple_of(j * R, R), R)
+        return pltpu.make_async_copy(t_ref.at[rows_j], y_ref.at[rows_j], fetch_sem.at[j])
+
+    def run(event, j):
+        (event1, event2, event3, event4, event5)[event - 1](j)
 
     load_x(0).start()
     load_g(0).start()
@@ -228,17 +245,11 @@
                     def _():
                         load_d(o).start()
 
-            @pl.when((i >= 1) & (t == 1))
-            def _():
-                @pl.when(i >= 2)
-                def _():
-                    event4(i - 2)
-
-                event1(i - 1)
-
-            @pl.when((i >= 1) & (t == nt - 1))
-            def _():
-                event2(i - 1)
+            for event, slot, lag in EVENTS:
+                if slot < nt:
+                    @pl.when((i >= lag) & (t == slot))
+                    def _():
+                        run(event, i - lag)
 
             return carry
 
@@ -262,12 +273,12 @@
                     s0(b).wait_send()
                     pl.semaphore_wait(credit0.at[b], 1)
 
-                v = _dot(hb[...], wd[o]).astype(BF16)
+                v = _dot(hb[...], y_ref[:, o * 2 * blk : (o + 1) * 2 * blk]).astype(BF16)
                 s0s[b, 0] = v[:, :blk]
                 s0s[b, 1] = v[:, blk:]
                 s0(b).start()
             else:
-                v = _dot(hb[...], wd[o])
+                v = _dot(hb[...], y_ref[:, o * 2 * blk : (o + 1) * 2 * blk])
                 s0(b).wait_recv()
                 lo = v[:, :blk] + s0r[b, 0].astype(F32)
                 hi = v[:, blk:] + s0r[b, 1].astype(F32)
@@ -289,31 +300,42 @@
                 def _():
                     pl.semaphore_signal(credit0.at[b], inc=1, device_id={"tp": partner}, device_id_type=MESH)
 
-        @pl.when(i >= 1)
-        def _():
-            event3(i - 1)
+            for event, slot, lag in EVENTS:
+                if slot == nt + o:
+                    @pl.when(i >= lag)
+                    def _():
+                        run(event, i - lag)
 
         return carry
 
     lax.fori_loop(0, nc, chunk, 0)
 
-    event1(nc - 1)
-    event4(nc - 2)
-    event2(nc - 1)
-    event3(nc - 1)
-    event4(nc - 1)
+    for b, to in enumerate((partner, n1, n2)):
+        pl.semaphore_signal(free.at[b], inc=1, device_id={"tp": to}, device_id_type=MESH)
+
+    def early(j, carry):
+        event5(j)
+        return carry
+
+    lax.fori_loop(0, nc - 3, early, 0)
+    rest = [(j + 4, 0, 5, j) for j in range(nc - 3, nc)]
+    for event, slot, lag in EVENTS:
+        for j in range(nc - lag, nc):
+            rest.append((j + lag, slot, event, j))
+    for _, _, event, j in sorted(rest):
+        run(event, j)
+
     for b in range(2):
         s0(b).wait_send()
     for j in (nc - 2, nc - 1):
         s1(j).wait_send()
         s2(j).wait_send()
-        wait_fins(j)
-
-    def last(j, carry):
-        finish(j)
+
+    def fetched(j, carry):
+        fetch(j).wait()
         return carry
 
-    lax.fori_loop(0, nc, last, 0)
+    lax.fori_loop(0, nc - 1, fetched, 0)
 
 
 def block(x, wg, wu, wd):
@@ -324,13 +346,12 @@
     dma, reg = pltpu.SemaphoreType.DMA, pltpu.SemaphoreType.REGULAR
     return pl.pallas_call(
         kernel,
-        out_shape=jax.ShapeDtypeStruct((rows, d), BF16),
+        out_shape=(pltpu.VMEM((rows, d), BF16), jax.ShapeDtypeStruct((rows, d), BF16)),
         in_specs=[hbm] * 4,
-        out_specs=hbm,
+        out_specs=(pl.BlockSpec(memory_space=pltpu.VMEM), hbm),
         scratch_shapes=[
             pltpu.VMEM((R, d), BF16),
             pltpu.VMEM((hid // GT, d, GT), BF16),
-            pltpu.VMEM((4, hid, 2 * blk), BF16),
             pltpu.VMEM((3, d // 2, GT), BF16),
             pltpu.VMEM((R, hid), BF16),
             pltpu.VMEM((2, 2, R, blk), BF16),
@@ -344,17 +365,17 @@
             pltpu.VMEM((2, R, blk), BF16),
             dma, dma((hid // GT,)), dma((4,)), dma((3,)),
             dma((2,)), dma((2,)), dma((2,)), dma((2,)), dma((2,)), dma((2,)),
-            dma((6, nc)), dma((6, nc)), dma((2,)),
-            reg((2,)), reg, reg,
+            dma((6, nc)), dma((6, nc)), dma((2,)), dma((nc,)),
+            reg((2,)), reg, reg, reg((3,)),
         ],
         compiler_params=pltpu.CompilerParams(
-            collective_id=0, has_side_effects=True, vmem_limit_bytes=67_043_328
+            collective_id=0, has_side_effects=True, vmem_limit_bytes=67_043_328 - 2 * rows * d
         ),
         cost_estimate=pl.CostEstimate(
             flops=6 * rows * d * hid, bytes_accessed=2 * (12 * d * hid), transcendentals=rows * hid
         ),
         name="mlp_all_reduce",
-    )(x, wg, wu, wd)
+    )(x, wg, wu, wd)[0]
 
 
 def solution(mesh):

time: 256 us -> 224 us (0.88)
  Pallas kernels: 239 us -> 216 us
  local copies, waits for them, and re-layouts: 17.3 us -> 7.54 us
    pallas_call x1, Pallas kernels: 239 us -> 216 us  [block(): pl.pallas_call(kernel, out_shape=(pltpu.VMEM((rows, d), BF16), jax.ShapeD...]
    unnamed x1, local copies, waits for them, and re-layouts: 17.3 us -> 7.54 us
where the time goes in v2:
time: 224 us
  Pallas kernels  216 us (96%)
  local copies, waits for them, and re-layouts  7.54 us (3%)
    pallas_call x1, Pallas kernels, block(): pl.pallas_call(kernel, out_shape=(pltpu.VMEM((rows, d), BF16), jax.ShapeD...  216 us
    unnamed x1, local copies, waits for them, and re-layouts  7.54 us

profile of v2, /device:TPU:0, one launch (start us, length us, event | category | flops | bytes accessed | tf_op | source)
XLA Modules:
  0.0 223.6 jit_solution(2264219972377550863)
XLA Ops:
  0.0 216.1 %mlp_all_reduce.1 = (bf16[2048,5120]{1,0:T(8,128)(2,1)S(1)}, bf16[2048,5120]{1,0:T(8,128)(2,1)}) custom-call(bf16[2048,5120]{1,0:T(8,128)(2,1)} %x_ref.1, bf16[5120,2048]{1,0:T(8,128)(2,1)} %wg_ref.1, bf16[5120,2048]{1,0:T(8,128)(2,1)} %wu_ref.1, bf16[2048,5120]{1,0:T(8,128)(2,1)} %wd_ref.1), custom_call_target="tpu_custom_call" | custom-call | flops 128849018880 | bytes 251658240 | tf_op jit(solution)/shard_map/mlp_all_reduce/pallas_call | solution.py:347
  216.1 7.5 %copy.6 = bf16[2048,5120]{1,0:T(8,128)(2,1)} copy(bf16[2048,5120]{1,0:T(8,128)(2,1)S(1)} %get-tuple-element.6) | data formatting | bytes 41943040

commit v3 on v2

--- a/solution.py
+++ b/solution.py
@@ -9,10 +9,14 @@
 
 MESH = pl.DeviceIdType.MESH
 R = 256
+RB = 64
+NT = 256
 GT = 512
 F32, BF16 = jnp.float32, jnp.bfloat16
 
-EVENTS = ((3, 1, 2), (1, 2, 1), (4, 4, 3), (2, 5, 1))
+EVENTS = ((1, 3, 1), (2, 0, 2), (3, 6, 2), (4, 5, 3))
+FIRST = ((1, 2, 1), (2, 4, 1), (3, 1, 2), (4, 4, 3))
+DRAIN = ((2, 1), (1, 0), (3, 1), (4, 2), (2, 0), (5, 2), (3, 0), (4, 1), (5, 1), (4, 0), (5, 0))
 
 
 def _dot(a, b):
@@ -31,9 +35,8 @@
     hid = wg_ref.shape[1]
     nc = rows // R
     nt = hid // GT
-    kh = d // 2
+    parts = [slice(k, k + R // 2) for k in (0, R // 2)]
     blk = d // 8
-    nring = 3
 
     me = lax.axis_index("tp")
     c = lax.rem(me, 2)
@@ -71,8 +74,8 @@
 
     order = (
         2 * (1 - c) + (1 - k2),
+        2 * (1 - c) + k2,
         2 * c + (1 - k1),
-        2 * (1 - c) + k2,
         2 * c + k1,
     )
 
@@ -81,22 +84,18 @@
         return pltpu.make_async_copy(wd_ref.at[:, pl.ds(col, 2 * blk)], y_ref.at[:, pl.ds(o * 2 * blk, 2 * blk)], wd_sem.at[o])
 
     def load_u(g):
-        s = lax.rem(g, 2 * nt)
-        t, half = s // 2, lax.rem(s, 2)
-        slot = lax.rem(g, nring)
-        src = wu_ref.at[pl.ds(pl.multiple_of(half * kh, kh), kh), pl.ds(pl.multiple_of(t * GT, 128), GT)]
+        t, slot = lax.rem(g, nt), lax.rem(g, 2)
+        src = wu_ref.at[:, pl.ds(pl.multiple_of(t * GT, 128), GT)]
         return pltpu.make_async_copy(src, ring.at[slot], ring_sem.at[slot])
 
     def s0(b):
         return remote(s0s.at[b], s0r.at[b], s0_ss.at[b], s0_rs.at[b], partner)
 
-    def s1(j):
-        p = lax.rem(j, 2)
-        return remote(s1s.at[p], s1r.at[p], s1_ss.at[p], s1_rs.at[p], n1)
-
-    def s2(j):
-        p = lax.rem(j, 2)
-        return remote(s2s.at[p], s2r.at[p], s2_ss.at[p], s2_rs.at[p], n2)
+    def s1():
+        return remote(s1s, s1r, s1_ss, s1_rs, n1)
+
+    def s2():
+        return remote(s2s, s2r, s2_ss, s2_rs, n2)
 
     def ag(kind, j, src, dst, to):
         return remote(src, dst, ag_ss.at[kind, j], ag_rs.at[kind, j], to)
@@ -126,39 +125,54 @@
         v = tile(j, 4 * c + 2 * (1 - k1), 2)
         return ag(5, j, v, v, partner)
 
+    def by_rows(f):
+        def body(q, carry):
+            f(pl.ds(pl.multiple_of(q * RB, RB), RB))
+            return carry
+
+        lax.fori_loop(0, R // RB, body, 0)
+
     def event1(j):
-        s1(j).wait_recv()
-        p = lax.rem(j, 2)
-
-        @pl.when(j >= 2)
+        s1().wait_recv()
+
+        @pl.when(j >= 1)
         def _():
-            s2(j).wait_send()
+            s2().wait_send()
             pl.semaphore_wait(credit2, 1)
 
-        s2s[p] = (keep1[1 - k2] + s1r[p, 1 - k2].astype(F32)).astype(BF16)
-        s2(j).start()
-        keep2[...] = keep1[k2] + s1r[p, k2].astype(F32)
-
-        @pl.when(j < nc - 2)
+        def send_half(q):
+            s2s[q] = (keep1[1 - k2, q] + s1r[1 - k2, q].astype(F32)).astype(BF16)
+
+        def keep_half(q):
+            keep2[q] = keep1[k2, q] + s1r[k2, q].astype(F32)
+
+        by_rows(send_half)
+        s2().start()
+        by_rows(keep_half)
+
+        @pl.when(j < nc - 1)
         def _():
             pl.semaphore_signal(credit1, inc=1, device_id={"tp": n1}, device_id_type=MESH)
 
     def event2(j):
-        s2(j).wait_recv()
+        s2().wait_recv()
         p = lax.rem(j, 2)
 
         @pl.when(j >= 2)
         def _():
             wait_fins(j - 2)
 
-        fin[p] = (keep2[...] + s2r[p].astype(F32)).astype(BF16)
+        def total(q):
+            fin[p, q] = (keep2[q] + s2r[q].astype(F32)).astype(BF16)
+
+        by_rows(total)
         if isinstance(j, int) and j == nc - 1:
             for b in range(3):
                 pl.semaphore_wait(free.at[b], 1)
         for cp in fins(j):
             cp.start()
 
-        @pl.when(j < nc - 2)
+        @pl.when(j < nc - 1)
         def _():
             pl.semaphore_signal(credit2, inc=1, device_id={"tp": n2}, device_id_type=MESH)
 
@@ -197,59 +211,71 @@
     def run(event, j):
         (event1, event2, event3, event4, event5)[event - 1](j)
 
+    def at_slot(slot, i, here):
+        for event, s, lag in FIRST:
+            if s == slot:
+                @pl.when(here & (i == lag))
+                def _():
+                    run(event, 0)
+
+        for event, s, lag in EVENTS:
+            if s == slot:
+                @pl.when(here & (i > lag))
+                def _():
+                    run(event, i - lag)
+
     load_x(0).start()
     load_g(0).start()
     load_u(0).start()
-    load_u(1).start()
-    load_g(1).start()
-    load_u(2).start()
 
     barrier = pltpu.get_barrier_semaphore()
     for to in (partner, n1, n2):
         pl.semaphore_signal(barrier, inc=1, device_id={"tp": to}, device_id_type=MESH)
     pl.semaphore_wait(barrier, 3)
 
+    def down(o, put):
+        for q in parts:
+            for lo in range(0, 2 * blk, NT):
+                v = _dot(hb[q], y_ref[:, o * 2 * blk + lo : o * 2 * blk + lo + NT])
+                for h in range(2):
+                    first, end = max(lo, h * blk), min(lo + NT, (h + 1) * blk)
+                    if first < end:
+                        put(h, q, slice(first - h * blk, end - h * blk), v[:, first - lo : end - lo])
+
     def chunk(i, carry):
         load_x(i).wait()
 
         def gate_up(t, carry):
-            g0 = 2 * nt * i + 2 * t
+            g = nt * i + t
 
             @pl.when(i == 0)
             def _():
                 load_g(t).wait()
 
-                @pl.when(t < nt - 2)
+                @pl.when(t < nt - 1)
                 def _():
-                    load_g(t + 2).start()
-
-            gate = _dot(xb[...], wg[t])
-            load_u(g0).wait()
-            load_u(g0 + 1).wait()
-            up = _dot(xb[:, :kh], ring[lax.rem(g0, nring)])
-            up += _dot(xb[:, kh:], ring[lax.rem(g0 + 1, nring)])
-            hb[:, pl.ds(pl.multiple_of(t * GT, 128), GT)] = (jax.nn.silu(gate) * up).astype(BF16)
-
-            @pl.when(g0 + 3 < 2 * nt * nc)
+                    load_g(t + 1).start()
+
+            load_u(g).wait()
+
+            @pl.when(g + 1 < nt * nc)
             def _():
-                load_u(g0 + 3).start()
-
-            @pl.when(g0 + 4 < 2 * nt * nc)
+                load_u(g + 1).start()
+
+            @pl.when((i == 0) & (t == nt - 1))
             def _():
-                load_u(g0 + 4).start()
-
-            @pl.when((i == 0) & (t >= nt - 2))
-            def _():
-                for o in range(2):
-                    @pl.when(t == nt - 2 + o)
-                    def _():
-                        load_d(o).start()
-
-            for event, slot, lag in EVENTS:
-                if slot < nt:
-                    @pl.when((i >= lag) & (t == slot))
-                    def _():
-                        run(event, i - lag)
+                for o in range(3):
+                    load_d(o).start()
+
+            cols = pl.ds(pl.multiple_of(t * GT, 128), GT)
+            slot = lax.rem(g, 2)
+            for q in parts:
+                gate = _dot(xb[q], wg[t])
+                up = _dot(xb[q], ring[slot])
+                hb[q, cols] = (jax.nn.silu(gate) * up).astype(BF16)
+
+            for slot in range(nt):
+                at_slot(slot, i, t == slot)
 
             return carry
 
@@ -263,48 +289,45 @@
             @pl.when(i == 0)
             def _():
                 load_d(o).wait()
-                if o < 2:
-                    load_d(o + 2).start()
-
-            b = o // 2
-            if o % 2 == 0:
+                if o == 0:
+                    load_d(3).start()
+
+            b = o % 2
+            if o < 2:
                 @pl.when(i >= 1)
                 def _():
                     s0(b).wait_send()
                     pl.semaphore_wait(credit0.at[b], 1)
 
-                v = _dot(hb[...], y_ref[:, o * 2 * blk : (o + 1) * 2 * blk]).astype(BF16)
-                s0s[b, 0] = v[:, :blk]
-                s0s[b, 1] = v[:, blk:]
+                def put(h, q, cols, v):
+                    s0s[b, h, q, cols] = v.astype(BF16)
+
+                down(o, put)
                 s0(b).start()
             else:
-                v = _dot(hb[...], y_ref[:, o * 2 * blk : (o + 1) * 2 * blk])
+                if o == 2:
+                    @pl.when(i >= 1)
+                    def _():
+                        s1().wait_send()
+                        pl.semaphore_wait(credit1, 1)
+
                 s0(b).wait_recv()
-                lo = v[:, :blk] + s0r[b, 0].astype(F32)
-                hi = v[:, blk:] + s0r[b, 1].astype(F32)
-                if o == 1:
-                    @pl.when(i >= 2)
-                    def _():
-                        s1(i).wait_send()
-                        pl.semaphore_wait(credit1, 1)
-
-                    p = lax.rem(i, 2)
-                    s1s[p, 0] = lo.astype(BF16)
-                    s1s[p, 1] = hi.astype(BF16)
-                    s1(i).start()
-                else:
-                    keep1[0] = lo
-                    keep1[1] = hi
+                def put(h, q, cols, v):
+                    v += s0r[b, h, q, cols].astype(F32)
+                    if o == 2:
+                        s1s[h, q, cols] = v.astype(BF16)
+                    else:
+                        keep1[h, q, cols] = v
+
+                down(o, put)
+                if o == 2:
+                    s1().start()
 
                 @pl.when(i < nc - 1)
                 def _():
                     pl.semaphore_signal(credit0.at[b], inc=1, device_id={"tp": partner}, device_id_type=MESH)
 
-            for event, slot, lag in EVENTS:
-                if slot == nt + o:
-                    @pl.when(i >= lag)
-                    def _():
-                        run(event, i - lag)
+            at_slot(nt + o, i, i >= 0)
 
         return carry
 
@@ -317,19 +340,15 @@
         event5(j)
         return carry
 
-    lax.fori_loop(0, nc - 3, early, 0)
-    rest = [(j + 4, 0, 5, j) for j in range(nc - 3, nc)]
-    for event, slot, lag in EVENTS:
-        for j in range(nc - lag, nc):
-            rest.append((j + lag, slot, event, j))
-    for _, _, event, j in sorted(rest):
-        run(event, j)
+    for k, (event, back) in enumerate(DRAIN):
+        run(event, nc - 1 - back)
+        if k == 0:
+            lax.fori_loop(0, nc - 3, early, 0)
 
     for b in range(2):
         s0(b).wait_send()
-    for j in (nc - 2, nc - 1):
-        s1(j).wait_send()
-        s2(j).wait_send()
+    s1().wait_send()
+    s2().wait_send()
 
     def fetched(j, carry):
         fetch(j).wait()
@@ -352,19 +371,19 @@
         scratch_shapes=[
             pltpu.VMEM((R, d), BF16),
             pltpu.VMEM((hid // GT, d, GT), BF16),
-            pltpu.VMEM((3, d // 2, GT), BF16),
+            pltpu.VMEM((2, d, GT), BF16),
             pltpu.VMEM((R, hid), BF16),
-            pltpu.VMEM((2, 2, R, blk), BF16),
-            pltpu.VMEM((2, 2, R, blk), BF16),
             pltpu.VMEM((2, 2, R, blk), BF16),
             pltpu.VMEM((2, 2, R, blk), BF16),
             pltpu.VMEM((2, R, blk), BF16),
             pltpu.VMEM((2, R, blk), BF16),
+            pltpu.VMEM((R, blk), BF16),
+            pltpu.VMEM((R, blk), BF16),
             pltpu.VMEM((2, R, blk), F32),
             pltpu.VMEM((R, blk), F32),
             pltpu.VMEM((2, R, blk), BF16),
-            dma, dma((hid // GT,)), dma((4,)), dma((3,)),
-            dma((2,)), dma((2,)), dma((2,)), dma((2,)), dma((2,)), dma((2,)),
+            dma, dma((hid // GT,)), dma((4,)), dma((2,)),
+            dma((2,)), dma((2,)), dma, dma, dma, dma,
             dma((6, nc)), dma((6, nc)), dma((2,)), dma((nc,)),
             reg((2,)), reg, reg, reg((3,)),
         ],

time: 224 us -> 218 us (0.973)
  Pallas kernels: 216 us -> 210 us
    pallas_call x1, Pallas kernels: 216 us -> 210 us  [block(): pl.pallas_call(kernel, out_shape=(pltpu.VMEM((rows, d), BF16), jax.ShapeD...]
where the time goes in v3:
time: 218 us
  Pallas kernels  210 us (96%)
  local copies, waits for them, and re-layouts  7.54 us (3%)
    pallas_call x1, Pallas kernels, block(): pl.pallas_call(kernel, out_shape=(pltpu.VMEM((rows, d), BF16), jax.ShapeD...  210 us
    unnamed x1, local copies, waits for them, and re-layouts  7.54 us

profile of v3, /device:TPU:0, one launch (start us, length us, event | category | flops | bytes accessed | tf_op | source)
XLA Modules:
  0.0 217.5 jit_solution(18168416246035999789)
XLA Ops:
  0.0 210.0 %mlp_all_reduce.1 = (bf16[2048,5120]{1,0:T(8,128)(2,1)S(1)}, bf16[2048,5120]{1,0:T(8,128)(2,1)}) custom-call(bf16[2048,5120]{1,0:T(8,128)(2,1)} %x_ref.1, bf16[5120,2048]{1,0:T(8,128)(2,1)} %wg_ref.1, bf16[5120,2048]{1,0:T(8,128)(2,1)} %wu_ref.1, bf16[2048,5120]{1,0:T(8,128)(2,1)} %wd_ref.1), custom_call_target="tpu_custom_call" | custom-call | flops 128849018880 | bytes 251658240 | tf_op jit(solution)/shard_map/mlp_all_reduce/pallas_call | solution.py:366
  210.0 7.5 %copy.6 = bf16[2048,5120]{1,0:T(8,128)(2,1)} copy(bf16[2048,5120]{1,0:T(8,128)(2,1)S(1)} %get-tuple-element.6) | data formatting | bytes 41943040

commit v4 on v3

--- a/solution.py
+++ b/solution.py
@@ -14,8 +14,7 @@
 GT = 512
 F32, BF16 = jnp.float32, jnp.bfloat16
 
-EVENTS = ((1, 3, 1), (2, 0, 2), (3, 6, 2), (4, 5, 3))
-FIRST = ((1, 2, 1), (2, 4, 1), (3, 1, 2), (4, 4, 3))
+EVENTS = ((10, 12, 18, 28), (11, 16, 22, 29))
 DRAIN = ((2, 1), (1, 0), (3, 1), (4, 2), (2, 0), (5, 2), (3, 0), (4, 1), (5, 1), (4, 0), (5, 0))
 
 
@@ -57,8 +56,11 @@
     p_mine_n2 = pc + 2 * k2 + (1 - k1)
     p_far = pc + 2 * (1 - k2)
 
+    def is_last(j):
+        return isinstance(j, int) and j == nc - 1
+
     def tile(j, b, n=1):
-        ref = y_ref if isinstance(j, int) and j == nc - 1 else t_ref
+        ref = y_ref if is_last(j) else t_ref
         return ref.at[pl.ds(pl.multiple_of(j * R, R), R), pl.ds(pl.multiple_of(b * blk, 128), n * blk)]
 
     def remote(src, dst, ss, rs, to):
@@ -122,8 +124,11 @@
         return ag(3, j, v, v, n1), ag(4, j, v, v, partner)
 
     def crossed(j):
+        if is_last(j):
+            va, vb = tile(j, far_a), tile(j, far_b)
+            return ag(5, j, va, va, partner), ag(6, j, vb, vb, partner)
         v = tile(j, 4 * c + 2 * (1 - k1), 2)
-        return ag(5, j, v, v, partner)
+        return (ag(5, j, v, v, partner),)
 
     def by_rows(f):
         def body(q, carry):
@@ -166,11 +171,14 @@
             fin[p, q] = (keep2[q] + s2r[q].astype(F32)).astype(BF16)
 
         by_rows(total)
-        if isinstance(j, int) and j == nc - 1:
+        if is_last(j):
             for b in range(3):
                 pl.semaphore_wait(free.at[b], 1)
-        for cp in fins(j):
-            cp.start()
+        a1, a2, a0, loc = fins(j)
+        a1.start()
+        a0.start()
+        loc.start()
+        a2.start()
 
         @pl.when(j < nc - 1)
         def _():
@@ -183,11 +191,14 @@
             cp.start()
 
     def event4(j):
+        sends = crossed(j)
         v = tile(j, far_a)
         ag(1, j, v, v, n1).wait_recv()
+        if is_last(j):
+            sends[0].start()
         v = tile(j, far_b)
         ag(3, j, v, v, n1).wait_recv()
-        crossed(j).start()
+        sends[-1].start()
 
     def event5(j):
         if isinstance(j, int) and j >= nc - 2:
@@ -196,12 +207,19 @@
         ag(2, j, v, v, partner).wait_recv()
         v = tile(j, p_mine_n2)
         ag(4, j, v, v, partner).wait_recv()
-        v = tile(j, p_far, 2)
-        ag(5, j, v, v, partner).wait_recv()
+        if is_last(j):
+            v = tile(j, p_far + k1)
+            ag(5, j, v, v, partner).wait_recv()
+            v = tile(j, p_far + (1 - k1))
+            ag(6, j, v, v, partner).wait_recv()
+        else:
+            v = tile(j, p_far, 2)
+            ag(5, j, v, v, partner).wait_recv()
         for cp in passed(j):
             cp.wait_send()
-        crossed(j).wait_send()
-        if not (isinstance(j, int) and j == nc - 1):
+        for cp in crossed(j):
+            cp.wait_send()
+        if not is_last(j):
             fetch(j).start()
 
     def fetch(j):
@@ -212,17 +230,15 @@
         (event1, event2, event3, event4, event5)[event - 1](j)
 
     def at_slot(slot, i, here):
-        for event, s, lag in FIRST:
-            if s == slot:
-                @pl.when(here & (i == lag))
-                def _():
-                    run(event, 0)
-
-        for event, s, lag in EVENTS:
-            if s == slot:
-                @pl.when(here & (i > lag))
-                def _():
-                    run(event, i - lag)
+        for first, row in enumerate(EVENTS):
+            for event, place in enumerate(row, 1):
+                if place % 8 == slot:
+                    j = i - place // 8
+                    mine_now = j >= first if first == len(EVENTS) - 1 else j == first
+
+                    @pl.when(here & mine_now)
+                    def _():
+                        run(event, j)
 
     load_x(0).start()
     load_g(0).start()
@@ -281,10 +297,6 @@
 
         lax.fori_loop(0, nt, gate_up, 0)
 
-        @pl.when(i < nc - 1)
-        def _():
-            load_x(i + 1).start()
-
         for o in range(4):
             @pl.when(i == 0)
             def _():
@@ -293,6 +305,11 @@
                     load_d(3).start()
 
             b = o % 2
+            if o == 2:
+                @pl.when(i < nc - 1)
+                def _():
+                    load_x(i + 1).start()
+
             if o < 2:
                 @pl.when(i >= 1)
                 def _():
@@ -340,10 +357,12 @@
         event5(j)
         return carry
 
-    for k, (event, back) in enumerate(DRAIN):
-        run(event, nc - 1 - back)
-        if k == 0:
+    lag_of = {event: place // 8 for event, place in enumerate(EVENTS[-1], 1)} | {5: nc}
+    for event, back in DRAIN:
+        if (event, back) == (3, 1):
             lax.fori_loop(0, nc - 3, early, 0)
+        if back < lag_of[event]:
+            run(event, nc - 1 - back)
 
     for b in range(2):
         s0(b).wait_send()
@@ -384,7 +403,7 @@
             pltpu.VMEM((2, R, blk), BF16),
             dma, dma((hid // GT,)), dma((4,)), dma((2,)),
             dma((2,)), dma((2,)), dma, dma, dma, dma,
-            dma((6, nc)), dma((6, nc)), dma((2,)), dma((nc,)),
+            dma((7, nc)), dma((7, nc)), dma((2,)), dma((nc,)),
             reg((2,)), reg, reg, reg((3,)),
         ],
         compiler_params=pltpu.CompilerParams(

time: 218 us -> 217 us (level)
  no operation moved by 1% of the time
where the time goes in v4:
time: 217 us
  Pallas kernels  209 us (96%)
  local copies, waits for them, and re-layouts  7.54 us (3%)
    pallas_call x1, Pallas kernels, block(): pl.pallas_call(kernel, out_shape=(pltpu.VMEM((rows, d), BF16), jax.ShapeD...  209 us
    unnamed x1, local copies, waits for them, and re-layouts  7.54 us

profile of v4, /device:TPU:0, one launch (start us, length us, event | category | flops | bytes accessed | tf_op | source)
XLA Modules:
  0.0 216.6 jit_solution(713307639631555276)
XLA Ops:
  0.0 209.1 %mlp_all_reduce.1 = (bf16[2048,5120]{1,0:T(8,128)(2,1)S(1)}, bf16[2048,5120]{1,0:T(8,128)(2,1)}) custom-call(bf16[2048,5120]{1,0:T(8,128)(2,1)} %x_ref.1, bf16[5120,2048]{1,0:T(8,128)(2,1)} %wg_ref.1, bf16[5120,2048]{1,0:T(8,128)(2,1)} %wu_ref.1, bf16[2048,5120]{1,0:T(8,128)(2,1)} %wd_ref.1), custom_call_target="tpu_custom_call" | custom-call | flops 128849018880 | bytes 251658240 | tf_op jit(solution)/shard_map/mlp_all_reduce/pallas_call | solution.py:385
  209.1 7.5 %copy.6 = bf16[2048,5120]{1,0:T(8,128)(2,1)} copy(bf16[2048,5120]{1,0:T(8,128)(2,1)S(1)} %get-tuple-element.6) | data formatting | bytes 41943040
